TPU v7x, 32 devices: a whole 2x2x4 slice. The times are simulated.
32 devices in a mesh: row: 4 (over y, x), col: 8 (over z, core).
Axes of the slice: x: 2, y: 2, z: 4, core: 2. Of those that a mesh axis runs over, the one named last changes fastest.
Arguments:
- tile_data: bfloat16 [128, 128, 128], P(('row', 'col')), may hold values from -24 to 24
- tile_coords: int32 [3, 128], P(None, ('row', 'col')), may hold values from 0 to 255, as said below
- tile_counts: int32 [32], P(('row', 'col')), may hold values from 1 to 4, as said below
- factor_rows: float32 [64, 8192], P(None, ('row', 'col')), may hold values from -6 to 6
- factor_cols: float32 [64, 16384], P(None, ('col', 'row')), may hold values from -6 to 6
- factor_depth: float32 [64, 256], P(None, ('row', 'col')), may hold values from -6 to 6
- damping: float32 [], replicated, may hold values from 64 to 256
Outputs:
- step_a: float32 [64, 8192], P(None, ('row', 'col'))
- step_b: float32 [64, 16384], P(None, ('col', 'row'))
- step_c: float32 [64, 256], P(None, ('row', 'col'))
Inputs may be any that keep to these rules, and one draw needn't show every extreme that they name: `tile_coords`: the first row names a tile's block within its device's group of 16 first-mode blocks, the second its block within the group of 16 second-mode blocks, the third its third-mode index below 256. `tile_counts`: slots at and beyond a device's count are padding and carry nothing; some device fills all 4 slots.
All inputs are finite; a program needn't handle non-finite values.
Results may differ from a plain program's by a relative error of at most 0.0003.
Values sent between devices are 32-bit elements; how exact they have to be, the bound alone decides.
A program may use at most 64 MiB of HBM per device.

v0:
```python
import jax
import jax.numpy as jnp
from jax import lax
from jax.sharding import PartitionSpec as P

RB = 16
CB = 16
ITERS = 2


exact_precision = lax.Precision.HIGHEST


def make_onehot(indices, block_count):
    return (indices[:, None] == jnp.arange(block_count, dtype=jnp.int32)[None, :]).astype(
        jnp.float32
    )


def pick_rows(onehot, blocks):
    shaped = blocks.reshape(blocks.shape[0], onehot.shape[1], blocks.shape[1] // onehot.shape[1])
    return jnp.einsum("tq,rqa->tra", onehot, shaped, precision=exact_precision)


def fold_rows(onehot, grads):
    summed = jnp.einsum("tq,tra->rqa", onehot, grads, precision=exact_precision)
    return summed.reshape(summed.shape[0], summed.shape[1] * summed.shape[2])


def tile_model(rows_a, rows_b, rows_c):
    return jnp.einsum(
        "tra,trb->tab", rows_a, rows_b * rows_c[:, :, None], precision=exact_precision
    )


def tile_products(rows_a, rows_b, rows_c, dir_a, dir_b, dir_c):
    depth_cols = rows_c[:, :, None]
    left_side = jnp.concatenate([dir_a, rows_a, rows_a], axis=1)
    right_side = jnp.concatenate(
        [rows_b * depth_cols, dir_b * depth_cols, rows_b * dir_c[:, :, None]], axis=1
    )
    return jnp.einsum("tra,trb->tab", left_side, right_side, precision=exact_precision)


def tile_transpose(values, rows_a, rows_b, rows_c):
    depth_cols = rows_c[:, :, None]
    row_raw = jnp.einsum("tab,trb->tra", values, rows_b, precision=exact_precision)
    grad_rows = row_raw * depth_cols
    grad_cols = jnp.einsum("tab,tra->trb", values, rows_a * depth_cols, precision=exact_precision)
    grad_depth = jnp.sum(rows_a * row_raw, axis=2)
    return (grad_rows, grad_cols, grad_depth)


def local_inner(first, second):
    return (
        jnp.sum(first[0] * second[0])
        + jnp.sum(first[1] * second[1])
        + jnp.sum(first[2] * second[2])
    )


def squares(residual):
    return lax.psum(local_inner(residual, residual), ("row", "col"))


def per_device(
    tile_data, tile_coords, tile_counts, factor_rows, factor_cols, factor_depth, damping
):
    whole_a = lax.all_gather(factor_rows, "col", axis=1, tiled=True)
    whole_b = lax.all_gather(factor_cols, "row", axis=1, tiled=True)
    whole_c = lax.all_gather(factor_depth, ("row", "col"), axis=1, tiled=True)
    piece_width = factor_depth.shape[1]
    own_start = lax.axis_index(("row", "col")) * piece_width
    live_mask = (jnp.arange(tile_data.shape[0], dtype=jnp.int32) < tile_counts[0]).astype(
        jnp.float32
    )[:, None, None]
    pick_a = make_onehot(tile_coords[0], RB)
    pick_b = make_onehot(tile_coords[1], CB)
    rows_a = pick_rows(pick_a, whole_a)
    rows_b = pick_rows(pick_b, whole_b)
    rows_c = jnp.take(whole_c, tile_coords[2], axis=1).T
    every_index = lax.all_gather(tile_coords[2], ("row", "col"), axis=0, tiled=True)

    def add_depth(piece):
        placed = (
            (every_index - own_start)[:, None] == jnp.arange(piece_width, dtype=jnp.int32)[None, :]
        ).astype(jnp.float32)
        return jnp.einsum("tr,tw->rw", piece, placed, precision=exact_precision)

    def send_back(values):
        grad_rows, grad_cols, grad_depth = tile_transpose(
            values * live_mask, rows_a, rows_b, rows_c
        )
        share_a = lax.psum_scatter(
            fold_rows(pick_a, grad_rows), "col", scatter_dimension=1, tiled=True
        )
        share_b = lax.psum_scatter(
            fold_rows(pick_b, grad_cols), "row", scatter_dimension=1, tiled=True
        )
        share_c = add_depth(lax.all_gather(grad_depth, ("row", "col"), axis=0, tiled=True))
        return (share_a, share_b, share_c)

    rhs = send_back(tile_data.astype(jnp.float32) - tile_model(rows_a, rows_b, rows_c))
    solution = tuple((jnp.zeros_like(member) for member in rhs))
    residual = rhs
    direction = rhs
    norm_now = squares(residual)
    for iteration in range(ITERS):
        gathered_a = lax.all_gather(direction[0], "col", axis=1, tiled=True)
        gathered_b = lax.all_gather(direction[1], "row", axis=1, tiled=True)
        gathered_c = lax.all_gather(direction[2], ("row", "col"), axis=1, tiled=True)
        hessian_values = tile_products(
            rows_a,
            rows_b,
            rows_c,
            pick_rows(pick_a, gathered_a),
            pick_rows(pick_b, gathered_b),
            jnp.take(gathered_c, tile_coords[2], axis=1).T,
        )
        applied = send_back(hessian_values)
        image_vec = tuple(
            (part_one + damping * part_two for part_one, part_two in zip(applied, direction))
        )
        curvature = lax.psum(local_inner(direction, image_vec), ("row", "col"))
        step_size = norm_now / curvature
        solution = tuple((sol + step_size * dvec for sol, dvec in zip(solution, direction)))
        residual = tuple((res - step_size * ivec for res, ivec in zip(residual, image_vec)))
        norm_next = squares(residual)
        direction = tuple(
            (res + norm_next / norm_now * dvec for res, dvec in zip(residual, direction))
        )
        norm_now = norm_next
    return (solution[0], solution[1], solution[2])


def solution(mesh):
    return jax.shard_map(
        per_device,
        mesh=mesh,
        in_specs=(
            P(("row", "col"), None, None),
            P(None, ("row", "col")),
            P(("row", "col")),
            P(None, ("row", "col")),
            P(None, ("col", "row")),
            P(None, ("row", "col")),
            P(),
        ),
        out_specs=(P(None, ("row", "col")), P(None, ("col", "row")), P(None, ("row", "col"))),
        check_vma=False,
    )
```

profile of v0, /device:TPU:0, one launch (start us, length us, event | category | flops | bytes accessed | tf_op | source)
XLA Modules:
  0.0 560.4 jit_solution(6114837716934857899)
XLA Ops:
  7.2 0.7 compare_and_fusion
  7.9 0.8 slice_bitcast_fusion
  8.7 44.0 %all_gather.41 = f32[64,256]{0,1:T(8,128)S(1)} all-gather(f32[64,8]{0,1:T(8,128)} %param.14), channel_id=1, replica_groups=mesh['row'=4,'col'=8] {'row','col'}, dimensions={1}, use_global_device_ids=true | all-gather | bytes 67584 | tf_op jit(solution)/shard_map/all_gather | solution.py:71
  52.6 0.6 gather_fusion
  53.5 9.3 %all_gather.39 = f32[64,2048]{1,0:T(8,128)S(1)} all-gather(f32[64,512]{1,0:T(8,128)S(1)} %copy-done.4), channel_id=1, replica_groups=mesh['row'=4,'col'=8] {'row'}, dimensions={1}, use_global_device_ids=true | all-gather | bytes 655360 | tf_op jit(solution)/shard_map/all_gather | solution.py:70
  62.9 0.7 copy-done.6
  63.7 14.9 %all_gather.40 = f32[64,2048]{1,0:T(8,128)S(1)} all-gather(f32[64,256]{1,0:T(8,128)S(1)} %copy-done.6), channel_id=1, replica_groups=mesh['row'=4,'col'=8] {'col'}, dimensions={1}, use_global_device_ids=true | all-gather | bytes 589824 | tf_op jit(solution)/shard_map/all_gather | solution.py:69
  79.7 0.3 broadcast_multiply_fusion.3
  80.0 0.6 copy-done.5
  80.6 0.6 fusion
  81.2 0.6 fusion.36
  81.8 0.5 fusion.21
  82.3 1.0 copy.121
  83.5 0.4 fusion.27
  83.9 0.5 fusion.13
  84.4 1.0 copy.120
  85.5 38.0 %all-gather.1 = f32[32,4,64]{2,1,0:T(4,128)S(1)} all-gather(f32[1,4,64]{2,1,0:T(4,128)S(1)} %copy.34), channel_id=1, replica_groups=mesh['row'=4,'col'=8] {'row','col'}, dimensions={0}, use_global_device_ids=true | all-gather | bytes 33792 | tf_op jit(solution)/shard_map/all_gather | solution.py:100
  123.5 0.8 bitcast_dynamic-update-slice_fusion
  124.3 38.2 %all-reduce = s32[128]{0:T(128)S(1)} all-reduce(s32[128]{0:T(128)S(1)} %bitcast_dynamic-update-slice_fusion), channel_id=2, replica_groups=mesh['row'=4,'col'=8] {'row','col'}, use_global_device_ids=true, to_apply=%add | all-reduce | flops 128 | bytes 1024
  162.8 41.1 %all_gather.46 = f32[64,256]{0,1:T(8,128)S(1)} all-gather(f32[64,8]{0,1:T(8,128)S(1)} %fusion.38), channel_id=1, replica_groups=mesh['row'=4,'col'=8] {'row','col'}, dimensions={1}, use_global_device_ids=true | all-gather | bytes 67584 | tf_op jit(solution)/shard_map/all_gather | solution.py:111
  203.9 0.6 gather_fusion.1
  204.8 15.1 %all_gather.44 = f32[64,2048]{1,0:T(8,128)S(1)} all-gather(f32[64,256]{1,0:T(8,128)} %reduce-scatter.7.cloned.1.call-done), channel_id=1, replica_groups=mesh['row'=4,'col'=8] {'col'}, dimensions={1}, use_global_device_ids=true | all-gather | bytes 589824 | tf_op jit(solution)/shard_map/all_gather | solution.py:109
  220.0 0.3 fusion.51
  220.4 10.3 %all_gather.45 = f32[64,2048]{1,0:T(8,128)S(1)} all-gather(f32[64,512]{1,0:T(8,128)} %reduce-scatter.9.cloned.1.call-done), channel_id=1, replica_groups=mesh['row'=4,'col'=8] {'row'}, dimensions={1}, use_global_device_ids=true | all-gather | bytes 655360 | tf_op jit(solution)/shard_map/all_gather | solution.py:110
  230.7 0.3 convolution_multiply_fusion.3
  231.2 1.0 convolution_multiply_fusion.1
  232.3 0.6 fusion.34
  232.9 0.5 fusion.19
  233.4 1.0 copy.119
  234.4 0.4 fusion.25
  234.7 0.5 fusion.11
  235.2 1.0 copy.118
  237.2 38.2 %all-gather.2 = f32[32,4,64]{2,1,0:T(4,128)S(1)} all-gather(f32[1,4,64]{2,1,0:T(4,128)S(1)} %copy.41), channel_id=1, replica_groups=mesh['row'=4,'col'=8] {'row','col'}, dimensions={0}, use_global_device_ids=true | all-gather | bytes 33792 | tf_op jit(solution)/shard_map/all_gather | solution.py:100
  275.4 1.0 multiply_reduce_fusion.12
  276.4 1.5 multiply_reduce_fusion.9
  277.8 11.3 %reduce-scatter.13.cloned.1.call-done = f32[64,512]{1,0:T(8,128)} async-done(((f32[64,2048]{1,0:T(8,128)}), f32[64,512]{1,0:T(8,128)}) %reduce-scatter.13.cloned.1.call-update) | async-done | bytes 131088 | tf_op jit(solution)/shard_map/reduce_scatter | solution.py:97
  289.1 1.6 multiply_reduce_fusion.4
  294.6 39.3 %all-reduce.1 = (f32[]{:T(128)}, f32[]{:T(128)}) all-reduce(f32[]{:T(128)S(6)} %add.88, f32[]{:T(128)S(6)} %add.93), channel_id=1, replica_groups=mesh['row'=4,'col'=8] {'row','col'}, use_global_device_ids=true, to_apply=%region_6.8 | all-reduce | flops 2 | bytes 16 | tf_op jit(solution)/shard_map/psum | solution.py:63
  335.2 0.7 multiply_reduce_fusion.11
  335.9 0.6 multiply_reduce_fusion.8
  336.5 0.6 multiply_reduce_fusion.2
  339.1 41.1 %psum.30 = f32[]{:T(128)} all-reduce(f32[]{:T(128)S(6)} %add.95), channel_id=1, replica_groups=mesh['row'=4,'col'=8] {'row','col'}, use_global_device_ids=true, to_apply=%region_17.19 | all-reduce | flops 1 | bytes 8 | tf_op jit(solution)/shard_map/psum | solution.py:63
  381.6 41.0 %all_gather.50 = f32[64,256]{0,1:T(8,128)S(1)} all-gather(f32[64,8]{0,1:T(8,128)S(1)} %multiply_add_fusion.7), channel_id=1, replica_groups=mesh['row'=4,'col'=8] {'row','col'}, dimensions={1}, use_global_device_ids=true | all-gather | bytes 67584 | tf_op jit(solution)/shard_map/all_gather | solution.py:111
  422.6 0.6 gather_fusion.2
  423.5 10.1 %all_gather.49 = f32[64,2048]{1,0:T(8,128)S(1)} all-gather(f32[64,512]{1,0:T(8,128)S(1)} %multiply_add_fusion.1), channel_id=1, replica_groups=mesh['row'=4,'col'=8] {'row'}, dimensions={1}, use_global_device_ids=true | all-gather | bytes 655360 | tf_op jit(solution)/shard_map/all_gather | solution.py:110
  433.7 0.3 convolution_multiply_fusion.2
  434.0 14.9 %all_gather.48 = f32[64,2048]{1,0:T(8,128)S(1)} all-gather(f32[64,256]{1,0:T(8,128)S(1)} %multiply_add_fusion.4), channel_id=1, replica_groups=mesh['row'=4,'col'=8] {'col'}, dimensions={1}, use_global_device_ids=true | all-gather | bytes 589824 | tf_op jit(solution)/shard_map/all_gather | solution.py:109
  449.1 0.3 fusion.48
  449.6 1.0 convolution_multiply_fusion
  450.6 0.6 fusion.32
  451.2 0.5 fusion.17
  451.7 1.0 copy.117
  452.7 0.4 fusion.23
  453.1 0.5 fusion.9
  453.6 1.0 copy.116
  454.8 37.9 %all-gather.3 = f32[32,4,64]{2,1,0:T(4,128)S(1)} all-gather(f32[1,4,64]{2,1,0:T(4,128)S(1)} %copy.48), channel_id=1, replica_groups=mesh['row'=4,'col'=8] {'row','col'}, dimensions={0}, use_global_device_ids=true | all-gather | bytes 33792 | tf_op jit(solution)/shard_map/all_gather | solution.py:100
  492.7 0.9 fusion.2
  493.6 1.5 multiply_reduce_fusion.7
  495.1 12.5 %reduce-scatter.17.cloned.1.call-done = f32[64,512]{1,0:T(8,128)} async-done(((f32[64,2048]{1,0:T(8,128)}), f32[64,512]{1,0:T(8,128)}) %reduce-scatter.17.cloned.1.call-update) | async-done | bytes 131088 | tf_op jit(solution)/shard_map/reduce_scatter | solution.py:97
  507.6 1.5 multiply_reduce_fusion.1
  511.0 39.3 %psum.31 = f32[]{:T(128)} all-reduce(f32[]{:T(128)S(6)} %add.103), channel_id=1, replica_groups=mesh['row'=4,'col'=8] {'row','col'}, use_global_device_ids=true, to_apply=%region_24.26 | all-reduce | flops 1 | bytes 8 | tf_op jit(solution)/shard_map/psum | solution.py:124
  551.6 0.6 multiply_add_fusion.6
  552.2 0.6 multiply_add_fusion.3
  552.9 0.7 multiply_add_fusion
  (60 shorter events, 3.7 us)
Async XLA Ops:
  7.2 197.6 %reduce-scatter.7.cloned.1.call-start = ((), (), s32[]{:S(2)}) async-start(), calls=%async_computation.6 | async-start | bytes 589824 | tf_op jit(solution)/shard_map/reduce_scatter | solution.py:94
  52.6 0.9 copy-start.4
  62.8 0.8 copy-start.6
  79.7 0.9 copy-start.5
  83.3 137.1 %reduce-scatter.9.cloned.1.call-start = ((), (), s32[]{:S(2)}) async-start(), calls=%async_computation.7 | async-start | bytes 655360 | tf_op jit(solution)/shard_map/reduce_scatter | solution.py:97
  85.4 191.0 %reduce-scatter.11.cloned.1.call-start = ((), (), s32[]{:S(2)}) async-start(), calls=%async_computation.8 | async-start | bytes 589824 | tf_op jit(solution)/shard_map/reduce_scatter | solution.py:94
  234.3 54.8 %reduce-scatter.13.cloned.1.call-start = ((), (), s32[]{:S(2)}) async-start(), calls=%async_computation.9 | async-start | bytes 655360 | tf_op jit(solution)/shard_map/reduce_scatter | solution.py:97
  236.2 257.4 %reduce-scatter.15.cloned.1.call-start = ((), (), s32[]{:S(2)}) async-start(), calls=%async_computation.10 | async-start | bytes 589824 | tf_op jit(solution)/shard_map/reduce_scatter | solution.py:94
  237.2 39.2 %copy-start.1 = (f32[64,256]{1,0:T(8,128)S(1)}, f32[64,256]{1,0:T(8,128)}, u32[]{:S(2)}) copy-start(f32[64,256]{1,0:T(8,128)} %reduce-scatter.7.cloned.1.call-done) | copy-start | bytes 196612
  275.4 13.7 %copy-start = (f32[64,512]{1,0:T(8,128)S(1)}, f32[64,512]{1,0:T(8,128)}, u32[]{:S(2)}) copy-start(f32[64,512]{1,0:T(8,128)} %reduce-scatter.9.cloned.1.call-done) | copy-start | bytes 393220
  289.1 46.8 %copy-start.3 = (f32[64,256]{1,0:T(8,128)S(1)}, f32[64,256]{1,0:T(8,128)}, u32[]{:S(2)}) copy-start(f32[64,256]{1,0:T(8,128)} %reduce-scatter.11.cloned.1.call-done) | copy-start | bytes 196612
  290.7 45.8 %copy-start.2 = (f32[64,512]{1,0:T(8,128)S(1)}, f32[64,512]{1,0:T(8,128)}, u32[]{:S(2)}) copy-start(f32[64,512]{1,0:T(8,128)} %reduce-scatter.13.cloned.1.call-done) | copy-start | bytes 393220
  452.7 54.9 %reduce-scatter.17.cloned.1.call-start = ((), (), s32[]{:S(2)}) async-start(), calls=%async_computation.11 | async-start | bytes 655360 | tf_op jit(solution)/shard_map/reduce_scatter | solution.py:97
Sparse Core Ops, SparseCore 0:
  83.4 28.6 reduce-scatter.6
  114.9 23.5 reduce-scatter.8
  234.5 28.7 reduce-scatter.10
  265.9 23.1 reduce-scatter.12
  452.8 28.6 reduce-scatter.14
  484.2 23.3 reduce-scatter.16
where the time goes:
time: 562 us; the launch traced here: 560 us
  blocking collectives  473 us (84%)
  between operations  27.4 us (5%)
  waiting for transfers between devices  23.9 us (4%)
  matrix products  12.5 us (2%)
  other arithmetic  12 us (2%)
  local copies, waits for them, and re-layouts  11.5 us (2%)
    all_gather x3, blocking collectives, send_back(): lax.all_gather(grad_depth, ('row', 'col'), axis=0, tiled=True)  114 us
    all_gather x2, blocking collectives, per_device(): lax.all_gather(direction[2], ('row', 'col'), axis=1, tiled=True)  82 us
    psum x2, blocking collectives, squares(): return lax.psum(local_inner(residual, residual), ('row', 'col'))  80.5 us
    all_gather x1, blocking collectives, per_device(): whole_c = lax.all_gather(factor_depth, ('row', 'col'), axis=1, tiled=True)  44 us
    psum x1, blocking collectives, per_device(): curvature = lax.psum(local_inner(direction, image_vec), ('row', 'col'))  39.3 us
    unnamed x1, blocking collectives  38.2 us
    all_gather x2, blocking collectives, per_device(): gathered_a = lax.all_gather(direction[0], 'col', axis=1, tiled=True)  30.1 us
    reduce_scatter x3, waiting for transfers between devices, send_back(): lax.psum_scatter(fold_rows(pick_b, grad_cols), 'row', scatter_dimension=1...  23.8 us
  transfers between devices with their start and end apart: 6, of which 2 were waited for; matrix products, arithmetic and copies ran while one was open for 2% of the time, Pallas kernels for 0%

commit v1 on v0

v1 whole, which is shorter than its diff:
```python
import functools

import jax
import jax.numpy as jnp
from jax import lax
from jax.experimental import pallas as pl
from jax.experimental.pallas import tpu as pltpu
from jax.sharding import PartitionSpec as P

MESH = pl.DeviceIdType.MESH
HI = lax.Precision.HIGHEST
F32 = jnp.float32


def dot(x, y, cx, cy):
    return lax.dot_general(
        x, y, (((cx,), (cy,)), ((), ())), precision=HI, preferred_element_type=F32
    )


def total(x):
    return jnp.sum(jnp.sum(x, axis=0, keepdims=True), axis=1, keepdims=True)


def kernel(
    nrow, ncol,
    tile, coords, counts, damp, fa, fb, fc,
    out_a, out_b, out_c,
    ga, gb, m1, ta1, tb1, m2, ta2, tb2, m3, s2, s3,
    pa, pb, pc, da, db, ra, rb, ia, ib, v0,
    send, recv,
):
    slots, size = tile.shape[0], tile.shape[1]
    rank = fa.shape[0]
    wc = fc.shape[0]
    ka, kb = fa.shape[1] // size, fb.shape[1] // size
    ndev = nrow * ncol
    p, q = lax.axis_index("row"), lax.axis_index("col")
    me = p * ncol + q

    def over_all(k):
        d = lax.rem(me + k, ndev)
        return (lax.div(d, ncol), lax.rem(d, ncol))

    def over_col(k):
        return (p, lax.rem(q + k, ncol))

    def over_row(k):
        return (lax.rem(p + k, nrow), q)

    def spread(src, dst, sem, n, where):
        def one(k, _):
            pltpu.make_async_remote_copy(
                src_ref=src, dst_ref=dst, send_sem=send.at[sem], recv_sem=recv.at[sem],
                device_id=where(k), device_id_type=MESH,
            ).start()
            return 0

        lax.fori_loop(1, n, one, 0)

    def arrived(buf, sem):
        part = buf.at[pl.ds(0, buf.shape[0] - 1)]
        pltpu.make_async_copy(part, part, recv.at[sem]).wait()

    def sent(buf, sem):
        part = buf.at[pl.ds(0, buf.shape[0] - 1)]
        pltpu.make_async_copy(part, part, send.at[sem]).wait()

    barrier = pltpu.get_barrier_semaphore()

    def greet(k, _):
        pl.semaphore_signal(barrier, inc=1, device_id=over_all(k), device_id_type=MESH)
        return 0

    lax.fori_loop(1, ndev, greet, 0)

    row_i = lax.broadcasted_iota(jnp.int32, (rank, 128), 0)
    lane_i = lax.broadcasted_iota(jnp.int32, (rank, 128), 1)
    eye = row_i == lane_i
    msg = m1.shape[1]
    mrow = lax.broadcasted_iota(jnp.int32, (msg, 128), 0)
    mlane = lax.broadcasted_iota(jnp.int32, (msg, 128), 1)

    def as_col(row):
        return jnp.sum(jnp.where(eye, row, 0.0), axis=1, keepdims=True)

    def as_row(col):
        return jnp.sum(jnp.where(eye, col, 0.0), axis=0, keepdims=True)

    first = jnp.where(mlane >= rank, -1.0, jnp.zeros((msg, 128), F32))
    for t in range(slots):
        for c in range(3):
            val = jnp.full((msg, 128), coords[c, t], jnp.int32).astype(F32)
            first = jnp.where((mrow == t) & (mlane == rank + c), val, first)
    m1[me] = first
    m1[me, :wc, :rank] = fc[...]
    for o in range(ka):
        ga[q, o] = fa[:, o * size : (o + 1) * size]
    for o in range(kb):
        gb[p, o] = fb[:, o * size : (o + 1) * size]

    pl.semaphore_wait(barrier, ndev - 1)
    spread(ga.at[q], ga.at[q], 0, ncol, over_col)
    spread(gb.at[p], gb.at[p], 1, nrow, over_row)
    spread(m1.at[me], m1.at[me], 2, ndev, over_all)
    arrived(m1, 2)

    def place(c, dst):
        def one(s, base):
            blk = m1[base + s]
            dst[s] = jnp.broadcast_to(blk[:, rank + c : rank + c + 1], (msg, 128))
            return base

        return one

    lax.fori_loop(0, ncol, place(0, pa), p * ncol)

    def place_b(s, _):
        blk = m1[s * ncol + q]
        pb[s] = jnp.broadcast_to(blk[:, rank + 1 : rank + 2], (msg, 128))
        return 0

    lax.fori_loop(0, nrow, place_b, 0)
    lax.fori_loop(0, ndev, place(2, pc), 0)

    arrived(ga, 0)
    arrived(gb, 1)

    count = counts[0]
    damping = damp[0]

    def splat(val):
        return jnp.full((1, 128), val, jnp.int32).astype(F32)

    my_a = [splat(coords[0, t]) for t in range(slots)]
    my_b = [splat(coords[1, t]) for t in range(slots)]
    my_c = [splat(coords[2, t]) for t in range(slots)]
    own_a = [splat(q * ka + o) for o in range(ka)]
    own_b = [splat(p * kb + o) for o in range(kb)]
    own_c = [splat(me * wc + o) for o in range(wc)]

    def tile_factors(t):
        a, b, k = coords[0, t], coords[1, t], coords[2, t]
        rows_a = ga[lax.div(a, ka), lax.rem(a, ka)]
        rows_b = gb[lax.div(b, kb), lax.rem(b, kb)]
        at = lax.div(k, wc)
        row_c = jnp.sum(jnp.where(mrow + at * wc == k, m1[at], 0.0), axis=0, keepdims=True)
        return rows_a, rows_b, as_col(row_c)

    facs = [tile_factors(t) for t in range(slots)]

    def send_grads(values, ta, tb, m, extra, sem):
        note = extra
        for t in range(slots):
            rows_a, rows_b, col_c = facs[t]
            raw = dot(rows_b, values[t], 1, 1)
            ta[q, t] = raw * col_c
            tb[p, t] = dot(rows_a * col_c, values[t], 1, 0)
            note = jnp.where(
                mrow == t, as_row(jnp.sum(rows_a * raw, axis=1, keepdims=True)), note
            )
        m[me] = note
        spread(ta.at[q], ta.at[q], sem, ncol, over_col)
        spread(tb.at[p], tb.at[p], sem + 1, nrow, over_row)
        spread(m.at[me], m.at[me], sem + 2, ndev, over_all)

    def live(t, x):
        return jnp.where(jnp.full((size, size), t, jnp.int32) < count, x, 0.0)

    values = [
        live(t, tile[t].astype(F32) - dot(facs[t][0], facs[t][1] * facs[t][2], 0, 0))
        for t in range(slots)
    ]
    send_grads(values, ta1, tb1, m2, jnp.zeros((msg, 128), F32), 3)

    def gather_sums(buf, place_ref, n, wanted):
        def one(s, accs):
            accs = list(accs)
            for t in range(slots):
                g = buf[s, t]
                tag = place_ref[s, t : t + 1, :]
                for j, want in enumerate(wanted):
                    accs[j] = accs[j] + g * jnp.where(tag == want, 1.0, 0.0)
            return tuple(accs)

        return lax.fori_loop(
            0, n, one, tuple(jnp.zeros((rank, size), F32) for _ in wanted)
        )

    def depth_sums(m, wanted):
        def one(s, accs):
            g, tag = m[s], pc[s]
            return tuple(acc + jnp.where(tag == w, g, 0.0) for acc, w in zip(accs, wanted))

        accs = lax.fori_loop(
            0, ndev, one, tuple(jnp.zeros((msg, 128), F32) for _ in wanted)
        )
        return [jnp.sum(acc, axis=0, keepdims=True) for acc in accs]

    arrived(ta1, 3)
    for t, x in enumerate(gather_sums(ta1, pa, ncol, my_a)):
        da[t] = x
    for o, x in enumerate(gather_sums(ta1, pa, ncol, own_a)):
        ra[o] = x
    arrived(tb1, 4)
    for t, x in enumerate(gather_sums(tb1, pb, nrow, my_b)):
        db[t] = x
    for o, x in enumerate(gather_sums(tb1, pb, nrow, own_b)):
        rb[o] = x
    arrived(m2, 5)
    depth = depth_sums(m2, my_c + own_c)
    dc, rc = depth[:slots], depth[slots:]

    def inner(xa, xb, xc, ya, yb, yc):
        part = jnp.zeros((rank, size), F32)
        for o in range(ka):
            part += xa(o) * ya(o)
        for o in range(kb):
            part += xb(o) * yb(o)
        res = total(part)
        for o in range(wc):
            res += total(xc[o] * yc[o])
        return res

    get_ra, get_rb = (lambda o: ra[o]), (lambda o: rb[o])
    norm_part = inner(get_ra, get_rb, rc, get_ra, get_rb, rc)

    def product(t, ua, ub, uc):
        rows_a, rows_b, col_c = facs[t]
        left = jnp.concatenate([ua, rows_a], axis=0)
        right = jnp.concatenate([rows_b * col_c, ub * col_c + rows_b * as_col(uc)], axis=0)
        return live(t, dot(left, right, 0, 0))

    curve = jnp.zeros((size, size), F32)
    values = []
    for t in range(slots):
        v = product(t, da[t], db[t], dc[t])
        v0[t] = v
        curve += v * v
        values.append(v)
    extra = jnp.where(
        mrow == slots, norm_part, jnp.where(mrow == slots + 1, total(curve), 0.0)
    )
    send_grads(values, ta2, tb2, m3, extra, 6)

    arrived(ta2, 6)
    for t, x in enumerate(gather_sums(ta2, pa, ncol, my_a)):
        ia[t] = x
    own_ia = gather_sums(ta2, pa, ncol, own_a)
    for o in range(ka):
        ia[slots + o] = own_ia[o]
    arrived(tb2, 7)
    for t, x in enumerate(gather_sums(tb2, pb, nrow, my_b)):
        ib[t] = x
    own_ib = gather_sums(tb2, pb, nrow, own_b)
    for o in range(kb):
        ib[slots + o] = own_ib[o]
    arrived(m3, 8)
    depth = depth_sums(m3, my_c + own_c)
    sums = jnp.sum(m3[...], axis=0)
    norm0 = sums[slots : slots + 1, :]
    curve0 = sums[slots + 1 : slots + 2, :]
    alpha0 = norm0 / (curve0 + damping * norm0)

    def next_residual(res, image):
        return res - alpha0 * (image + damping * res)

    for o in range(ka):
        ia[slots + o] = next_residual(ra[o], ia[slots + o])
    for o in range(kb):
        ib[slots + o] = next_residual(rb[o], ib[slots + o])
    rc1 = [next_residual(rc[o], depth[slots + o]) for o in range(wc)]
    get_a1, get_b1 = (lambda o: ia[slots + o]), (lambda o: ib[slots + o])
    fresh_part = inner(get_a1, get_b1, rc1, get_a1, get_b1, rc1)
    cross_part = inner(get_a1, get_b1, rc1, get_ra, get_rb, rc)
    two = lax.broadcasted_iota(jnp.int32, (2, 128), 0)
    s2[me] = jnp.where(two == 0, fresh_part, cross_part)
    spread(s2.at[me], s2.at[me], 9, ndev, over_all)

    values = [
        product(
            t,
            next_residual(da[t], ia[t]),
            next_residual(db[t], ib[t]),
            next_residual(dc[t], depth[t]),
        )
        for t in range(slots)
    ]
    arrived(s2, 9)
    sums = jnp.sum(s2[...], axis=0)
    fresh, cross = sums[0:1, :], sums[1:2, :]
    beta = fresh / norm0
    curve = jnp.zeros((size, size), F32)
    for t in range(slots):
        v = values[t] + beta * v0[t]
        curve += v * v
    s3[me] = jnp.broadcast_to(total(curve), (1, 128))
    spread(s3.at[me], s3.at[me], 10, ndev, over_all)
    direct = fresh + 2.0 * beta * cross + beta * beta * norm0
    arrived(s3, 10)
    curve1 = jnp.sum(s3[...], axis=0)
    alpha1 = fresh / (curve1 + damping * direct)

    def step(res, res1):
        return alpha0 * res + alpha1 * (res1 + beta * res)

    for o in range(ka):
        out_a[:, o * size : (o + 1) * size] = step(ra[o], ia[slots + o])
    for o in range(kb):
        out_b[:, o * size : (o + 1) * size] = step(rb[o], ib[slots + o])
    for o in range(wc):
        out_c[o : o + 1, :] = step(rc[o], rc1[o])[:, :rank]

    for i, buf in enumerate((ga, gb, m1, ta1, tb1, m2, ta2, tb2, m3, s2, s3)):
        sent(buf, i)


def per_device(
    nrow, ncol, tile_data, tile_coords, tile_counts, factor_rows, factor_cols, factor_depth, damping
):
    slots, size, _ = tile_data.shape
    rank, wa = factor_rows.shape
    wb, wc = factor_cols.shape[1], factor_depth.shape[1]
    ka, kb = wa // size, wb // size
    ndev = nrow * ncol
    msg = -(-max(wc, slots + 2) // 8) * 8
    vm = pltpu.VMEM
    exchange = [
        vm((ncol, slots, rank, size), F32),
        vm((nrow, slots, rank, size), F32),
        vm((ndev, msg, 128), F32),
    ]
    vspec = pl.BlockSpec(memory_space=pltpu.VMEM)
    sspec = pl.BlockSpec(memory_space=pltpu.SMEM)
    step_a, step_b, step_c = pl.pallas_call(
        functools.partial(kernel, nrow, ncol),
        out_shape=(
            jax.ShapeDtypeStruct((rank, wa), F32),
            jax.ShapeDtypeStruct((rank, wb), F32),
            jax.ShapeDtypeStruct((wc, rank), F32),
        ),
        in_specs=[vspec, sspec, sspec, sspec, vspec, vspec, vspec],
        out_specs=(vspec, vspec, vspec),
        scratch_shapes=[
            vm((ncol, ka, rank, size), F32),
            vm((nrow, kb, rank, size), F32),
            vm((ndev, msg, 128), F32),
            *exchange,
            *exchange,
            vm((ndev, 2, 128), F32),
            vm((ndev, 1, 128), F32),
            vm((ncol, msg, 128), F32),
            vm((nrow, msg, 128), F32),
            vm((ndev, msg, 128), F32),
            vm((slots, rank, size), F32),
            vm((slots, rank, size), F32),
            vm((ka, rank, size), F32),
            vm((kb, rank, size), F32),
            vm((slots + ka, rank, size), F32),
            vm((slots + kb, rank, size), F32),
            vm((slots, size, size), F32),
            pltpu.SemaphoreType.DMA((11,)),
            pltpu.SemaphoreType.DMA((11,)),
        ],
        compiler_params=pltpu.CompilerParams(collective_id=0, has_side_effects=True),
    )(
        tile_data, tile_coords, tile_counts, damping.reshape(1),
        factor_rows, factor_cols, factor_depth.T,
    )
    return step_a, step_b, step_c.T


def solution(mesh):
    nrow, ncol = mesh.shape["row"], mesh.shape["col"]
    return jax.shard_map(
        functools.partial(per_device, nrow, ncol),
        mesh=mesh,
        in_specs=(
            P(("row", "col"), None, None),
            P(None, ("row", "col")),
            P(("row", "col")),
            P(None, ("row", "col")),
            P(None, ("col", "row")),
            P(None, ("row", "col")),
            P(),
        ),
        out_specs=(P(None, ("row", "col")), P(None, ("col", "row")), P(None, ("row", "col"))),
        check_vma=False,
    )
```

time: 562 us -> 101 us (0.18)
  blocking collectives: 473 us -> 0 us
  Pallas kernels: 0 us -> 95.8 us
  between operations: 27.4 us -> 1.94 us
  waiting for transfers between devices: 23.9 us -> 0 us
  matrix products: 12.5 us -> 0 us
  other arithmetic: 12 us -> 0 us
  local copies, waits for them, and re-layouts: 11.5 us -> 2.78 us
    all_gather x12 -> x0, blocking collectives: 315 us -> none  [the longest x3 114 us: send_back(): lax.all_gather(grad_depth, ('row', 'col'), axis=0, tiled=True)]
    psum x3 -> x0, blocking collectives: 120 us -> none  [the longest x2 80.5 us: squares(): return lax.psum(local_inner(residual, residual), ('row', 'col'))]
    pallas_call x0 -> x1, Pallas kernels: none -> 95.8 us  [per_device(): pl.pallas_call(functools.partial(kernel, nrow, ncol), out_shape=(jax.Shap...]
    unnamed x1 -> x0, blocking collectives: 38.2 us -> none
    reduce_scatter x6 -> x0, waiting for transfers between devices: 23.8 us -> none  [the longest x3 23.8 us: send_back(): lax.psum_scatter(fold_rows(pick_b, grad_cols), 'row', scatter_dimension=1...]
    dot_general x24 -> x0, matrix products: 12.5 us -> none  [the longest x6 2.95 us: fold_rows(): summed = jnp.einsum('tq,tra->rqa', onehot, grads, precision=exact_precision)]
    reduce_sum x9 -> x0, other arithmetic: 8.34 us -> none  [the longest x3 3.79 us: local_inner(): jnp.sum(first[1] * second[1])]
    unnamed x31 -> x7, local copies, waits for them, and re-layouts: 8.82 us -> 2.78 us
  transfers between devices with their start and end apart: 6 -> 0, of which waited for: 2 -> 0; matrix products, arithmetic and copies ran while one was open for 2% -> 0% of each run, Pallas kernels for 0% -> 0%
where the time goes in v1:
time: 101 us
  Pallas kernels  95.8 us (95%)
  local copies, waits for them, and re-layouts  2.78 us (3%)
  between operations  1.94 us (2%)
    pallas_call x1, Pallas kernels, per_device(): pl.pallas_call(functools.partial(kernel, nrow, ncol), out_shape=(jax.Shap...  95.8 us
    unnamed x7, local copies, waits for them, and re-layouts  2.78 us

profile of v1, /device:TPU:0, one launch (start us, length us, event | category | flops | bytes accessed | tf_op | source)
XLA Modules:
  0.0 100.6 jit_solution(9038425880647923837)
XLA Ops:
  1.9 95.8 %shard_map.94 = (f32[64,256]{1,0:T(8,128)}, f32[64,512]{1,0:T(8,128)}, f32[8,64]{1,0:T(8,128)}) custom-call(bf16[4,128,128]{2,1,0:T(8,128)(2,1)} %tile.1, s32[3,4]{1,0:T(4,128)} %coords.1, s32[1]{0:T(128)S(6)} %copy.13.counts, f32[1]{0:T(128)} %bitcast.3.damp, f32[64,256]{1,0:T(8,128)} %fa.1, f32[64,512]{1,0:T(8,128)} %fb.1, f32[8,64]{1,0:T(8,128)} %bitcast.5), custom_call_target="tpu_custom_call" | custom-call | tf_op jit(solution)/shard_map/pallas_call | solution.py:335
  97.8 0.0 copy-start
  97.8 1.5 %copy.15 = f32[64,256]{1,0:T(8,128)} copy(f32[64,256]{1,0:T(8,128)} %get-tuple-element.12) | data formatting | bytes 131072
  99.3 0.0 copy-done
  99.3 0.0 copy-start.1
  99.3 0.7 copy.16
  100.0 0.0 copy-done.1
  100.0 0.6 copy.17
Async XLA Ops:
  97.8 1.5 %copy-start = (f32[64,512]{1,0:T(8,128)S(1)}, f32[64,512]{1,0:T(8,128)}, u32[]{:S(2)}) copy-start(f32[64,512]{1,0:T(8,128)} %get-tuple-element.13) | copy-start | bytes 393220
  99.3 0.7 copy-start.1

commit v2 on v1

--- a/solution.py
+++ b/solution.py
@@ -8,6 +8,7 @@
 from jax.sharding import PartitionSpec as P
 
 MESH = pl.DeviceIdType.MESH
+CORES = 2
 HI = lax.Precision.HIGHEST
 F32 = jnp.float32
 
@@ -28,7 +29,7 @@
     out_a, out_b, out_c,
     ga, gb, m1, ta1, tb1, m2, ta2, tb2, m3, s2, s3,
     pa, pb, pc, da, db, ra, rb, ia, ib, v0,
-    send, recv,
+    send, recv, ls0, lr0, ls1, lr1, ls2, lr2,
 ):
     slots, size = tile.shape[0], tile.shape[1]
     rank = fa.shape[0]
@@ -66,6 +67,89 @@
         part = buf.at[pl.ds(0, buf.shape[0] - 1)]
         pltpu.make_async_copy(part, part, send.at[sem]).wait()
 
+    nz = ncol // CORES
+    z, core = lax.div(q, CORES), lax.rem(q, CORES)
+    other = CORES - 1 - core
+
+    def move(buf, ls, lr, dz, block, chunk):
+        target = (q + CORES, q - CORES, z * CORES + other)[dz]
+        piece = buf.at[block * CORES + core, chunk]
+        return pltpu.make_async_remote_copy(
+            src_ref=piece, dst_ref=piece,
+            send_sem=ls.at[dz, block, chunk], recv_sem=lr.at[block * CORES + core, chunk],
+            device_id=(p, target), device_id_type=MESH,
+        )
+
+    def line_start(buf, ls, lr):
+        for chunk in range(buf.shape[1]):
+            @pl.when(z + 1 < nz)
+            def _():
+                move(buf, ls, lr, 0, z, chunk).start()
+
+            @pl.when(z > 0)
+            def _():
+                move(buf, ls, lr, 1, z, chunk).start()
+
+            move(buf, ls, lr, 2, z, chunk).start()
+
+    def line_relay(buf, ls, lr):
+        chunks = buf.shape[1]
+
+        def landed(slot, chunk):
+            piece = buf.at[slot, chunk]
+            pltpu.make_async_copy(piece, piece, lr.at[slot, chunk]).wait()
+
+        def one(d, _):
+            for chunk in range(chunks):
+                @pl.when(z - d >= 0)
+                def _():
+                    block = z - d
+                    landed(block * CORES + core, chunk)
+
+                    @pl.when(z + 1 < nz)
+                    def _():
+                        move(buf, ls, lr, 0, block, chunk).start()
+
+                    move(buf, ls, lr, 2, block, chunk).start()
+
+                @pl.when(z + d < nz)
+                def _():
+                    block = z + d
+                    landed(block * CORES + core, chunk)
+
+                    @pl.when(z > 0)
+                    def _():
+                        move(buf, ls, lr, 1, block, chunk).start()
+
+                    move(buf, ls, lr, 2, block, chunk).start()
+
+            return 0
+
+        lax.fori_loop(1, nz, one, 0)
+
+        def rest(block, _):
+            for chunk in range(chunks):
+                landed(block * CORES + other, chunk)
+            return 0
+
+        lax.fori_loop(0, nz, rest, 0)
+
+    def line_sent(buf, ls, lr):
+        def one(block, _):
+            for chunk in range(buf.shape[1]):
+                @pl.when((z + 1 < nz) & (block <= z))
+                def _():
+                    move(buf, ls, lr, 0, block, chunk).wait_send()
+
+                @pl.when((z > 0) & (block >= z))
+                def _():
+                    move(buf, ls, lr, 1, block, chunk).wait_send()
+
+                move(buf, ls, lr, 2, block, chunk).wait_send()
+            return 0
+
+        lax.fori_loop(0, nz, one, 0)
+
     barrier = pltpu.get_barrier_semaphore()
 
     def greet(k, _):
@@ -80,6 +164,8 @@
     msg = m1.shape[1]
     mrow = lax.broadcasted_iota(jnp.int32, (msg, 128), 0)
     mlane = lax.broadcasted_iota(jnp.int32, (msg, 128), 1)
+    nrow_i = lax.broadcasted_iota(jnp.int32, (slots, 128), 0)
+    nlane = lax.broadcasted_iota(jnp.int32, (slots, 128), 1)
 
     def as_col(row):
         return jnp.sum(jnp.where(eye, row, 0.0), axis=1, keepdims=True)
@@ -100,9 +186,10 @@
         gb[p, o] = fb[:, o * size : (o + 1) * size]
 
     pl.semaphore_wait(barrier, ndev - 1)
-    spread(ga.at[q], ga.at[q], 0, ncol, over_col)
+    spread(m1.at[me], m1.at[me], 2, ndev, over_all)
+    line_start(ga, ls0, lr0)
     spread(gb.at[p], gb.at[p], 1, nrow, over_row)
-    spread(m1.at[me], m1.at[me], 2, ndev, over_all)
+    line_relay(ga, ls0, lr0)
     arrived(m1, 2)
 
     def place(c, dst):
@@ -123,7 +210,6 @@
     lax.fori_loop(0, nrow, place_b, 0)
     lax.fori_loop(0, ndev, place(2, pc), 0)
 
-    arrived(ga, 0)
     arrived(gb, 1)
 
     count = counts[0]
@@ -149,7 +235,7 @@
 
     facs = [tile_factors(t) for t in range(slots)]
 
-    def send_grads(values, ta, tb, m, extra, sem):
+    def send_grads(values, ta, tb, m, extra, sem, ls, lr):
         note = extra
         for t in range(slots):
             rows_a, rows_b, col_c = facs[t]
@@ -157,12 +243,13 @@
             ta[q, t] = raw * col_c
             tb[p, t] = dot(rows_a * col_c, values[t], 1, 0)
             note = jnp.where(
-                mrow == t, as_row(jnp.sum(rows_a * raw, axis=1, keepdims=True)), note
+                (nrow_i == t) & (nlane < rank),
+                as_row(jnp.sum(rows_a * raw, axis=1, keepdims=True)), note,
             )
         m[me] = note
-        spread(ta.at[q], ta.at[q], sem, ncol, over_col)
+        spread(m.at[me], m.at[me], sem + 2, ndev, over_all)
+        line_start(ta, ls, lr)
         spread(tb.at[p], tb.at[p], sem + 1, nrow, over_row)
-        spread(m.at[me], m.at[me], sem + 2, ndev, over_all)
 
     def live(t, x):
         return jnp.where(jnp.full((size, size), t, jnp.int32) < count, x, 0.0)
@@ -171,7 +258,7 @@
         live(t, tile[t].astype(F32) - dot(facs[t][0], facs[t][1] * facs[t][2], 0, 0))
         for t in range(slots)
     ]
-    send_grads(values, ta1, tb1, m2, jnp.zeros((msg, 128), F32), 3)
+    send_grads(values, ta1, tb1, m2, jnp.zeros((slots, 128), F32), 3, ls1, lr1)
 
     def gather_sums(buf, place_ref, n, wanted):
         def one(s, accs):
@@ -189,15 +276,17 @@
 
     def depth_sums(m, wanted):
         def one(s, accs):
-            g, tag = m[s], pc[s]
+            g, tag = m[s], pc[s, :slots]
             return tuple(acc + jnp.where(tag == w, g, 0.0) for acc, w in zip(accs, wanted))
 
         accs = lax.fori_loop(
-            0, ndev, one, tuple(jnp.zeros((msg, 128), F32) for _ in wanted)
+            0, ndev, one, tuple(jnp.zeros((slots, 128), F32) for _ in wanted)
         )
-        return [jnp.sum(acc, axis=0, keepdims=True) for acc in accs]
-
-    arrived(ta1, 3)
+        return [
+            jnp.sum(jnp.where(nlane < rank, acc, 0.0), axis=0, keepdims=True) for acc in accs
+        ]
+
+    line_relay(ta1, ls1, lr1)
     for t, x in enumerate(gather_sums(ta1, pa, ncol, my_a)):
         da[t] = x
     for o, x in enumerate(gather_sums(ta1, pa, ncol, own_a)):
@@ -239,11 +328,11 @@
         curve += v * v
         values.append(v)
     extra = jnp.where(
-        mrow == slots, norm_part, jnp.where(mrow == slots + 1, total(curve), 0.0)
+        nlane == rank, norm_part, jnp.where(nlane == rank + 1, total(curve), 0.0)
     )
-    send_grads(values, ta2, tb2, m3, extra, 6)
-
-    arrived(ta2, 6)
+    send_grads(values, ta2, tb2, m3, extra, 6, ls2, lr2)
+
+    line_relay(ta2, ls2, lr2)
     for t, x in enumerate(gather_sums(ta2, pa, ncol, my_a)):
         ia[t] = x
     own_ia = gather_sums(ta2, pa, ncol, own_a)
@@ -258,8 +347,8 @@
     arrived(m3, 8)
     depth = depth_sums(m3, my_c + own_c)
     sums = jnp.sum(m3[...], axis=0)
-    norm0 = sums[slots : slots + 1, :]
-    curve0 = sums[slots + 1 : slots + 2, :]
+    norm0 = jnp.broadcast_to(sums[0:1, rank : rank + 1], (1, 128))
+    curve0 = jnp.broadcast_to(sums[0:1, rank + 1 : rank + 2], (1, 128))
     alpha0 = norm0 / (curve0 + damping * norm0)
 
     def next_residual(res, image):
@@ -311,7 +400,10 @@
     for o in range(wc):
         out_c[o : o + 1, :] = step(rc[o], rc1[o])[:, :rank]
 
-    for i, buf in enumerate((ga, gb, m1, ta1, tb1, m2, ta2, tb2, m3, s2, s3)):
+    line_sent(ga, ls0, lr0)
+    line_sent(ta1, ls1, lr1)
+    line_sent(ta2, ls2, lr2)
+    for i, buf in ((1, gb), (2, m1), (4, tb1), (5, m2), (7, tb2), (8, m3), (9, s2), (10, s3)):
         sent(buf, i)
 
 
@@ -323,13 +415,20 @@
     wb, wc = factor_cols.shape[1], factor_depth.shape[1]
     ka, kb = wa // size, wb // size
     ndev = nrow * ncol
-    msg = -(-max(wc, slots + 2) // 8) * 8
+    msg = -(-max(wc, slots) // 8) * 8
     vm = pltpu.VMEM
     exchange = [
         vm((ncol, slots, rank, size), F32),
         vm((nrow, slots, rank, size), F32),
-        vm((ndev, msg, 128), F32),
+        vm((ndev, slots, 128), F32),
     ]
+
+    def line(chunks):
+        return [
+            pltpu.SemaphoreType.DMA((3, ncol // CORES, chunks)),
+            pltpu.SemaphoreType.DMA((ncol, chunks)),
+        ]
+
     vspec = pl.BlockSpec(memory_space=pltpu.VMEM)
     sspec = pl.BlockSpec(memory_space=pltpu.SMEM)
     step_a, step_b, step_c = pl.pallas_call(
@@ -361,6 +460,9 @@
             vm((slots, size, size), F32),
             pltpu.SemaphoreType.DMA((11,)),
             pltpu.SemaphoreType.DMA((11,)),
+            *line(ka),
+            *line(slots),
+            *line(slots),
         ],
         compiler_params=pltpu.CompilerParams(collective_id=0, has_side_effects=True),
     )(

time: 101 us -> 70.4 us (0.70)
  Pallas kernels: 95.8 us -> 65.5 us
    pallas_call x1, Pallas kernels: 95.8 us -> 65.5 us  [per_device(): pl.pallas_call(functools.partial(kernel, nrow, ncol), out_shape=(jax.Shap...]
where the time goes in v2:
time: 70.4 us; the launch traced here: 70.2 us
  Pallas kernels  65.5 us (93%)
  local copies, waits for them, and re-layouts  2.78 us (4%)
  between operations  1.94 us (3%)
    pallas_call x1, Pallas kernels, per_device(): pl.pallas_call(functools.partial(kernel, nrow, ncol), out_shape=(jax.Shap...  65.5 us
    unnamed x7, local copies, waits for them, and re-layouts  2.78 us

profile of v2, /device:TPU:0, one launch (start us, length us, event | category | flops | bytes accessed | tf_op | source)
XLA Modules:
  0.0 70.2 jit_solution(9872546220562218958)
XLA Ops:
  1.9 65.5 %shard_map.94 = (f32[64,256]{1,0:T(8,128)}, f32[64,512]{1,0:T(8,128)}, f32[8,64]{1,0:T(8,128)}) custom-call(bf16[4,128,128]{2,1,0:T(8,128)(2,1)} %tile.1, s32[3,4]{1,0:T(4,128)} %coords.1, s32[1]{0:T(128)S(6)} %copy.13.counts, f32[1]{0:T(128)} %bitcast.3.damp, f32[64,256]{1,0:T(8,128)} %fa.1, f32[64,512]{1,0:T(8,128)} %fb.1, f32[8,64]{1,0:T(8,128)} %bitcast.5), custom_call_target="tpu_custom_call" | custom-call | tf_op jit(solution)/shard_map/pallas_call | solution.py:434
  67.4 0.0 copy-start
  67.4 1.5 %copy.15 = f32[64,256]{1,0:T(8,128)} copy(f32[64,256]{1,0:T(8,128)} %get-tuple-element.12) | data formatting | bytes 131072
  69.0 0.0 copy-done
  69.0 0.0 copy-start.1
  69.0 0.7 copy.16
  69.6 0.0 copy-done.1
  69.6 0.6 copy.17
Async XLA Ops:
  67.4 1.5 %copy-start = (f32[64,512]{1,0:T(8,128)S(1)}, f32[64,512]{1,0:T(8,128)}, u32[]{:S(2)}) copy-start(f32[64,512]{1,0:T(8,128)} %get-tuple-element.13) | copy-start | bytes 393220
  69.0 0.7 copy-start.1

commit v3 on v2

--- a/solution.py
+++ b/solution.py
@@ -27,8 +27,8 @@
     nrow, ncol,
     tile, coords, counts, damp, fa, fb, fc,
     out_a, out_b, out_c,
-    ga, gb, m1, ta1, tb1, m2, ta2, tb2, m3, s2, s3,
-    pa, pb, pc, da, db, ra, rb, ia, ib, v0,
+    ga, gb, m1, ta1, tb1, m2, ta2, tb2, m3, s2,
+    pa, pb, pc, da, db, ia, ib, v0,
     send, recv, ls0, lr0, ls1, lr1, ls2, lr2,
 ):
     slots, size = tile.shape[0], tile.shape[1]
@@ -80,8 +80,8 @@
             device_id=(p, target), device_id_type=MESH,
         )
 
-    def line_start(buf, ls, lr):
-        for chunk in range(buf.shape[1]):
+    def line_start(buf, ls, lr, chunks):
+        for chunk in chunks:
             @pl.when(z + 1 < nz)
             def _():
                 move(buf, ls, lr, 0, z, chunk).start()
@@ -92,15 +92,15 @@
 
             move(buf, ls, lr, 2, z, chunk).start()
 
-    def line_relay(buf, ls, lr):
-        chunks = buf.shape[1]
+    def line_relay(buf, ls, lr, use, between):
+        chunks = range(buf.shape[1])
 
         def landed(slot, chunk):
             piece = buf.at[slot, chunk]
             pltpu.make_async_copy(piece, piece, lr.at[slot, chunk]).wait()
 
-        def one(d, _):
-            for chunk in range(chunks):
+        def relay(d):
+            for chunk in chunks:
                 @pl.when(z - d >= 0)
                 def _():
                     block = z - d
@@ -123,16 +123,37 @@
 
                     move(buf, ls, lr, 2, block, chunk).start()
 
+                @pl.when(z - d >= 0)
+                def _():
+                    use((z - d) * CORES + core, chunk)
+
+                @pl.when(z + d < nz)
+                def _():
+                    use((z + d) * CORES + core, chunk)
+
+        def partner(d):
+            for chunk in chunks:
+                @pl.when(z - d >= 0)
+                def _():
+                    landed((z - d) * CORES + other, chunk)
+                    use((z - d) * CORES + other, chunk)
+
+                @pl.when((z + d < nz) & (d > 0))
+                def _():
+                    landed((z + d) * CORES + other, chunk)
+                    use((z + d) * CORES + other, chunk)
+
+        def stage(d, _):
+            relay(d)
+            partner(d - 1)
             return 0
 
-        lax.fori_loop(1, nz, one, 0)
-
-        def rest(block, _):
-            for chunk in range(chunks):
-                landed(block * CORES + other, chunk)
-            return 0
-
-        lax.fori_loop(0, nz, rest, 0)
+        for chunk in chunks:
+            use(q, chunk)
+        lax.fori_loop(1, nz - 1, stage, 0)
+        between()
+        lax.fori_loop(nz - 1, nz, stage, 0)
+        partner(nz - 1)
 
     def line_sent(buf, ls, lr):
         def one(block, _):
@@ -187,10 +208,8 @@
 
     pl.semaphore_wait(barrier, ndev - 1)
     spread(m1.at[me], m1.at[me], 2, ndev, over_all)
-    line_start(ga, ls0, lr0)
+    line_start(ga, ls0, lr0, range(ka))
     spread(gb.at[p], gb.at[p], 1, nrow, over_row)
-    line_relay(ga, ls0, lr0)
-    arrived(m1, 2)
 
     def place(c, dst):
         def one(s, base):
@@ -200,17 +219,20 @@
 
         return one
 
-    lax.fori_loop(0, ncol, place(0, pa), p * ncol)
 
     def place_b(s, _):
         blk = m1[s * ncol + q]
         pb[s] = jnp.broadcast_to(blk[:, rank + 1 : rank + 2], (msg, 128))
         return 0
 
-    lax.fori_loop(0, nrow, place_b, 0)
-    lax.fori_loop(0, ndev, place(2, pc), 0)
-
-    arrived(gb, 1)
+    def place_all():
+        arrived(m1, 2)
+        lax.fori_loop(0, ncol, place(0, pa), p * ncol)
+        lax.fori_loop(0, nrow, place_b, 0)
+        lax.fori_loop(0, ndev, place(2, pc), 0)
+        arrived(gb, 1)
+
+    line_relay(ga, ls0, lr0, lambda slot, chunk: None, place_all)
 
     count = counts[0]
     damping = damp[0]
@@ -241,6 +263,7 @@
             rows_a, rows_b, col_c = facs[t]
             raw = dot(rows_b, values[t], 1, 1)
             ta[q, t] = raw * col_c
+            line_start(ta, ls, lr, (t,))
             tb[p, t] = dot(rows_a * col_c, values[t], 1, 0)
             note = jnp.where(
                 (nrow_i == t) & (nlane < rank),
@@ -248,7 +271,6 @@
             )
         m[me] = note
         spread(m.at[me], m.at[me], sem + 2, ndev, over_all)
-        line_start(ta, ls, lr)
         spread(tb.at[p], tb.at[p], sem + 1, nrow, over_row)
 
     def live(t, x):
@@ -260,19 +282,34 @@
     ]
     send_grads(values, ta1, tb1, m2, jnp.zeros((slots, 128), F32), 3, ls1, lr1)
 
-    def gather_sums(buf, place_ref, n, wanted):
-        def one(s, accs):
-            accs = list(accs)
+    def take(acc, buf, tags, wanted):
+        def one(slot, chunk):
+            g = buf[slot, chunk]
+            tag = tags[slot, chunk : chunk + 1, :]
+            for i, want in enumerate(wanted):
+                acc[i] += g * jnp.where(tag == want, 1.0, 0.0)
+
+        return one
+
+    def collect(ta, tb, m, ls, lr, sem, acc_a, acc_b):
+        acc_a[...] = jnp.zeros_like(acc_a)
+        acc_b[...] = jnp.zeros_like(acc_b)
+        take_b = take(acc_b, tb, pb, my_b + own_b)
+        depth = []
+
+        def row_sums(s, _):
             for t in range(slots):
-                g = buf[s, t]
-                tag = place_ref[s, t : t + 1, :]
-                for j, want in enumerate(wanted):
-                    accs[j] = accs[j] + g * jnp.where(tag == want, 1.0, 0.0)
-            return tuple(accs)
-
-        return lax.fori_loop(
-            0, n, one, tuple(jnp.zeros((rank, size), F32) for _ in wanted)
-        )
+                take_b(s, t)
+            return 0
+
+        def between():
+            arrived(m, sem + 2)
+            depth.extend(depth_sums(m, my_c + own_c))
+            arrived(tb, sem + 1)
+            lax.fori_loop(0, nrow, row_sums, 0)
+
+        line_relay(ta, ls, lr, take(acc_a, ta, pa, my_a + own_a), between)
+        return depth
 
     def depth_sums(m, wanted):
         def one(s, accs):
@@ -286,18 +323,7 @@
             jnp.sum(jnp.where(nlane < rank, acc, 0.0), axis=0, keepdims=True) for acc in accs
         ]
 
-    line_relay(ta1, ls1, lr1)
-    for t, x in enumerate(gather_sums(ta1, pa, ncol, my_a)):
-        da[t] = x
-    for o, x in enumerate(gather_sums(ta1, pa, ncol, own_a)):
-        ra[o] = x
-    arrived(tb1, 4)
-    for t, x in enumerate(gather_sums(tb1, pb, nrow, my_b)):
-        db[t] = x
-    for o, x in enumerate(gather_sums(tb1, pb, nrow, own_b)):
-        rb[o] = x
-    arrived(m2, 5)
-    depth = depth_sums(m2, my_c + own_c)
+    depth = collect(ta1, tb1, m2, ls1, lr1, 3, da, db)
     dc, rc = depth[:slots], depth[slots:]
 
     def inner(xa, xb, xc, ya, yb, yc):
@@ -311,7 +337,7 @@
             res += total(xc[o] * yc[o])
         return res
 
-    get_ra, get_rb = (lambda o: ra[o]), (lambda o: rb[o])
+    get_ra, get_rb = (lambda o: da[slots + o]), (lambda o: db[slots + o])
     norm_part = inner(get_ra, get_rb, rc, get_ra, get_rb, rc)
 
     def product(t, ua, ub, uc):
@@ -332,20 +358,7 @@
     )
     send_grads(values, ta2, tb2, m3, extra, 6, ls2, lr2)
 
-    line_relay(ta2, ls2, lr2)
-    for t, x in enumerate(gather_sums(ta2, pa, ncol, my_a)):
-        ia[t] = x
-    own_ia = gather_sums(ta2, pa, ncol, own_a)
-    for o in range(ka):
-        ia[slots + o] = own_ia[o]
-    arrived(tb2, 7)
-    for t, x in enumerate(gather_sums(tb2, pb, nrow, my_b)):
-        ib[t] = x
-    own_ib = gather_sums(tb2, pb, nrow, own_b)
-    for o in range(kb):
-        ib[slots + o] = own_ib[o]
-    arrived(m3, 8)
-    depth = depth_sums(m3, my_c + own_c)
+    depth = collect(ta2, tb2, m3, ls2, lr2, 6, ia, ib)
     sums = jnp.sum(m3[...], axis=0)
     norm0 = jnp.broadcast_to(sums[0:1, rank : rank + 1], (1, 128))
     curve0 = jnp.broadcast_to(sums[0:1, rank + 1 : rank + 2], (1, 128))
@@ -355,55 +368,50 @@
         return res - alpha0 * (image + damping * res)
 
     for o in range(ka):
-        ia[slots + o] = next_residual(ra[o], ia[slots + o])
+        ia[slots + o] = next_residual(da[slots + o], ia[slots + o])
     for o in range(kb):
-        ib[slots + o] = next_residual(rb[o], ib[slots + o])
+        ib[slots + o] = next_residual(db[slots + o], ib[slots + o])
     rc1 = [next_residual(rc[o], depth[slots + o]) for o in range(wc)]
     get_a1, get_b1 = (lambda o: ia[slots + o]), (lambda o: ib[slots + o])
     fresh_part = inner(get_a1, get_b1, rc1, get_a1, get_b1, rc1)
     cross_part = inner(get_a1, get_b1, rc1, get_ra, get_rb, rc)
-    two = lax.broadcasted_iota(jnp.int32, (2, 128), 0)
-    s2[me] = jnp.where(two == 0, fresh_part, cross_part)
-    spread(s2.at[me], s2.at[me], 9, ndev, over_all)
-
-    values = [
-        product(
+    curve_part = jnp.zeros((size, size), F32)
+    mixed_part = jnp.zeros((size, size), F32)
+    for t in range(slots):
+        v = product(
             t,
             next_residual(da[t], ia[t]),
             next_residual(db[t], ib[t]),
             next_residual(dc[t], depth[t]),
         )
-        for t in range(slots)
-    ]
+        curve_part += v * v
+        mixed_part += v * v0[t]
+    parts = (fresh_part, cross_part, total(curve_part), total(mixed_part))
+    for i, part in enumerate(parts):
+        s2[me, i : i + 1, :] = jnp.broadcast_to(part, (1, 128))
+    spread(s2.at[me], s2.at[me], 9, ndev, over_all)
     arrived(s2, 9)
     sums = jnp.sum(s2[...], axis=0)
-    fresh, cross = sums[0:1, :], sums[1:2, :]
+    fresh, cross, curve_r, mixed = (sums[i : i + 1, :] for i in range(4))
     beta = fresh / norm0
-    curve = jnp.zeros((size, size), F32)
-    for t in range(slots):
-        v = values[t] + beta * v0[t]
-        curve += v * v
-    s3[me] = jnp.broadcast_to(total(curve), (1, 128))
-    spread(s3.at[me], s3.at[me], 10, ndev, over_all)
-    direct = fresh + 2.0 * beta * cross + beta * beta * norm0
-    arrived(s3, 10)
-    curve1 = jnp.sum(s3[...], axis=0)
+    direct = fresh + beta * (2.0 * cross + beta * norm0)
+    curve1 = curve_r + beta * (2.0 * mixed + beta * curve0)
     alpha1 = fresh / (curve1 + damping * direct)
 
     def step(res, res1):
         return alpha0 * res + alpha1 * (res1 + beta * res)
 
     for o in range(ka):
-        out_a[:, o * size : (o + 1) * size] = step(ra[o], ia[slots + o])
+        out_a[:, o * size : (o + 1) * size] = step(da[slots + o], ia[slots + o])
     for o in range(kb):
-        out_b[:, o * size : (o + 1) * size] = step(rb[o], ib[slots + o])
+        out_b[:, o * size : (o + 1) * size] = step(db[slots + o], ib[slots + o])
     for o in range(wc):
         out_c[o : o + 1, :] = step(rc[o], rc1[o])[:, :rank]
 
     line_sent(ga, ls0, lr0)
     line_sent(ta1, ls1, lr1)
     line_sent(ta2, ls2, lr2)
-    for i, buf in ((1, gb), (2, m1), (4, tb1), (5, m2), (7, tb2), (8, m3), (9, s2), (10, s3)):
+    for i, buf in ((1, gb), (2, m1), (4, tb1), (5, m2), (7, tb2), (8, m3), (9, s2)):
         sent(buf, i)
 
 
@@ -446,20 +454,17 @@
             vm((ndev, msg, 128), F32),
             *exchange,
             *exchange,
-            vm((ndev, 2, 128), F32),
-            vm((ndev, 1, 128), F32),
+            vm((ndev, 4, 128), F32),
             vm((ncol, msg, 128), F32),
             vm((nrow, msg, 128), F32),
             vm((ndev, msg, 128), F32),
-            vm((slots, rank, size), F32),
-            vm((slots, rank, size), F32),
-            vm((ka, rank, size), F32),
-            vm((kb, rank, size), F32),
+            vm((slots + ka, rank, size), F32),
+            vm((slots + kb, rank, size), F32),
             vm((slots + ka, rank, size), F32),
             vm((slots + kb, rank, size), F32),
             vm((slots, size, size), F32),
-            pltpu.SemaphoreType.DMA((11,)),
-            pltpu.SemaphoreType.DMA((11,)),
+            pltpu.SemaphoreType.DMA((10,)),
+            pltpu.SemaphoreType.DMA((10,)),
             *line(ka),
             *line(slots),
             *line(slots),

time: 70.4 us -> 58.7 us (0.83)
  Pallas kernels: 65.5 us -> 53.8 us
    pallas_call x1, Pallas kernels: 65.5 us -> 53.8 us  [per_device(): pl.pallas_call(functools.partial(kernel, nrow, ncol), out_shape=(jax.Shap...]
where the time goes in v3:
time: 58.7 us; the launch traced here: 58.5 us
  Pallas kernels  53.8 us (92%)
  local copies, waits for them, and re-layouts  2.78 us (5%)
  between operations  1.94 us (3%)
    pallas_call x1, Pallas kernels, per_device(): pl.pallas_call(functools.partial(kernel, nrow, ncol), out_shape=(jax.Shap...  53.8 us
    unnamed x7, local copies, waits for them, and re-layouts  2.78 us

profile of v3, /device:TPU:0, one launch (start us, length us, event | category | flops | bytes accessed | tf_op | source)
XLA Modules:
  0.0 58.5 jit_solution(15623961480994767676)
XLA Ops:
  1.9 53.8 %shard_map.94 = (f32[64,256]{1,0:T(8,128)}, f32[64,512]{1,0:T(8,128)}, f32[8,64]{1,0:T(8,128)}) custom-call(bf16[4,128,128]{2,1,0:T(8,128)(2,1)} %tile.1, s32[3,4]{1,0:T(4,128)} %coords.1, s32[1]{0:T(128)S(6)} %copy.13.counts, f32[1]{0:T(128)} %bitcast.3.damp, f32[64,256]{1,0:T(8,128)} %fa.1, f32[64,512]{1,0:T(8,128)} %fb.1, f32[8,64]{1,0:T(8,128)} %bitcast.5), custom_call_target="tpu_custom_call" | custom-call | tf_op jit(solution)/shard_map/pallas_call | solution.py:442
  55.7 0.0 copy-start
  55.7 1.5 %copy.15 = f32[64,256]{1,0:T(8,128)} copy(f32[64,256]{1,0:T(8,128)} %get-tuple-element.12) | data formatting | bytes 131072
  57.2 0.0 copy-done
  57.2 0.0 copy-start.1
  57.2 0.7 %copy.16 = f32[64,512]{1,0:T(8,128)} copy(f32[64,512]{1,0:T(8,128)S(1)} %copy-done) | data formatting | bytes 262144
  57.9 0.0 copy-done.1
  57.9 0.6 %copy.17 = f32[64,8]{0,1:T(8,128)} copy(f32[64,8]{0,1:T(8,128)S(1)} %bitcast.4) | data formatting | bytes 4096
Async XLA Ops:
  55.7 1.5 %copy-start = (f32[64,512]{1,0:T(8,128)S(1)}, f32[64,512]{1,0:T(8,128)}, u32[]{:S(2)}) copy-start(f32[64,512]{1,0:T(8,128)} %get-tuple-element.13) | copy-start | bytes 393220
  57.2 0.7 %copy-start.1 = (f32[8,64]{1,0:T(8,128)S(1)}, f32[8,64]{1,0:T(8,128)}, u32[]{:S(2)}) copy-start(f32[8,64]{1,0:T(8,128)} %get-tuple-element.8) | copy-start | bytes 6148

commit v4 on v3

--- a/solution.py
+++ b/solution.py
@@ -29,7 +29,7 @@
     out_a, out_b, out_c,
     ga, gb, m1, ta1, tb1, m2, ta2, tb2, m3, s2,
     pa, pb, pc, da, db, ia, ib, v0,
-    send, recv, ls0, lr0, ls1, lr1, ls2, lr2,
+    gate, send, recv, ls0, lr0, ls1, lr1, ls2, lr2,
 ):
     slots, size = tile.shape[0], tile.shape[1]
     rank = fa.shape[0]
@@ -173,11 +173,10 @@
 
     barrier = pltpu.get_barrier_semaphore()
 
-    def greet(k, _):
-        pl.semaphore_signal(barrier, inc=1, device_id=over_all(k), device_id_type=MESH)
-        return 0
-
-    lax.fori_loop(1, ndev, greet, 0)
+    for k in range(1, nrow):
+        pl.semaphore_signal(barrier, inc=1, device_id=over_row(k), device_id_type=MESH)
+    for k in range(1, ncol):
+        pl.semaphore_signal(barrier, inc=1, device_id=over_col(k), device_id_type=MESH)
 
     row_i = lax.broadcasted_iota(jnp.int32, (rank, 128), 0)
     lane_i = lax.broadcasted_iota(jnp.int32, (rank, 128), 1)
@@ -206,10 +205,13 @@
     for o in range(kb):
         gb[p, o] = fb[:, o * size : (o + 1) * size]
 
-    pl.semaphore_wait(barrier, ndev - 1)
-    spread(m1.at[me], m1.at[me], 2, ndev, over_all)
+    pl.semaphore_wait(barrier, nrow + ncol - 2)
+    for k in range(1, nrow):
+        pl.semaphore_signal(gate, inc=1, device_id=over_row(k), device_id_type=MESH)
     line_start(ga, ls0, lr0, range(ka))
     spread(gb.at[p], gb.at[p], 1, nrow, over_row)
+    pl.semaphore_wait(gate, nrow - 1)
+    spread(m1.at[me], m1.at[me], 2, ndev, over_all)
 
     def place(c, dst):
         def one(s, base):
@@ -463,6 +465,7 @@
             vm((slots + ka, rank, size), F32),
             vm((slots + kb, rank, size), F32),
             vm((slots, size, size), F32),
+            pltpu.SemaphoreType.REGULAR,
             pltpu.SemaphoreType.DMA((10,)),
             pltpu.SemaphoreType.DMA((10,)),
             *line(ka),

time: 58.7 us -> 58.3 us (level)
  no operation moved by 1% of the time
where the time goes in v4:
time: 58.3 us; the launch traced here: 58.1 us
  Pallas kernels  53.4 us (92%)
  local copies, waits for them, and re-layouts  2.78 us (5%)
  between operations  1.94 us (3%)
    pallas_call x1, Pallas kernels, per_device(): pl.pallas_call(functools.partial(kernel, nrow, ncol), out_shape=(jax.Shap...  53.4 us
    unnamed x7, local copies, waits for them, and re-layouts  2.78 us

profile of v4, /device:TPU:0, one launch (start us, length us, event | category | flops | bytes accessed | tf_op | source)
XLA Modules:
  0.0 58.1 jit_solution(1902813519224291103)
XLA Ops:
  1.9 53.4 %shard_map.94 = (f32[64,256]{1,0:T(8,128)}, f32[64,512]{1,0:T(8,128)}, f32[8,64]{1,0:T(8,128)}) custom-call(bf16[4,128,128]{2,1,0:T(8,128)(2,1)} %tile.1, s32[3,4]{1,0:T(4,128)} %coords.1, s32[1]{0:T(128)S(6)} %copy.13.counts, f32[1]{0:T(128)} %bitcast.3.damp, f32[64,256]{1,0:T(8,128)} %fa.1, f32[64,512]{1,0:T(8,128)} %fb.1, f32[8,64]{1,0:T(8,128)} %bitcast.5), custom_call_target="tpu_custom_call" | custom-call | tf_op jit(solution)/shard_map/pallas_call | solution.py:444
  55.3 0.0 copy-start
  55.3 1.5 %copy.15 = f32[64,256]{1,0:T(8,128)} copy(f32[64,256]{1,0:T(8,128)} %get-tuple-element.12) | data formatting | bytes 131072
  56.8 0.0 copy-done
  56.8 0.0 copy-start.1
  56.8 0.7 %copy.16 = f32[64,512]{1,0:T(8,128)} copy(f32[64,512]{1,0:T(8,128)S(1)} %copy-done) | data formatting | bytes 262144
  57.5 0.0 copy-done.1
  57.5 0.6 %copy.17 = f32[64,8]{0,1:T(8,128)} copy(f32[64,8]{0,1:T(8,128)S(1)} %bitcast.4) | data formatting | bytes 4096
Async XLA Ops:
  55.3 1.5 %copy-start = (f32[64,512]{1,0:T(8,128)S(1)}, f32[64,512]{1,0:T(8,128)}, u32[]{:S(2)}) copy-start(f32[64,512]{1,0:T(8,128)} %get-tuple-element.13) | copy-start | bytes 393220
  56.8 0.7 %copy-start.1 = (f32[8,64]{1,0:T(8,128)S(1)}, f32[8,64]{1,0:T(8,128)}, u32[]{:S(2)}) copy-start(f32[8,64]{1,0:T(8,128)} %get-tuple-element.8) | copy-start | bytes 6148
